TPU v7x, 32 devices: a whole 2x2x4 slice. The times are simulated.
32 devices in a mesh: dp: 8 (over y, x, core), mp: 4 (over z).
Axes of the slice: x: 2, y: 2, z: 4, core: 2. Of those that a mesh axis runs over, the one named last changes fastest.
Arguments:
- tokens: bfloat16 [1024, 8192], P(('dp', 'mp')), parts along dimension 0, may hold values from -6 to 6
- norm_gain: float32 [8192], replicated, may hold values from 0.5 to 1.5
- qkv_weight: bfloat16 [8192, 10240], P(None, 'mp'), may hold values from -0.0625 to 0.0625
- qkv_bias: float32 [10240], P('mp'), may hold values from -3 to 3
- qkv_grad: bfloat16 [1024, 10240], P('dp', 'mp'), parts along dimension 0, may hold values from -6 to 6
Outputs:
- qkv: bfloat16 [1024, 10240], P('dp', 'mp'), parts along dimension 0
- tokens_grad: float32 [1024, 8192], P(('dp', 'mp')), parts along dimension 0
- gain_grad: float32 [65536], P('dp'), parts along dimension 0
- bias_grad: float32 [81920], P(('dp', 'mp')), parts along dimension 0
There are 8 independent parts, one for each index of `dp`. A program takes and returns all parts, laid end to end along the dimension named above; an argument that names none is the same for every part. Nothing has to cross between parts.
All inputs are finite; a program needn't handle non-finite values.
Results may differ from a plain program's by a relative error of at most 0.0046.
Values may be sent and summed in bfloat16 or wider, within the bound.
A program may use at most 128 MiB of HBM per device.

v0:
```python
import jax
import jax.numpy as jnp
from jax import lax
from jax.sharding import PartitionSpec as P

HEAD_DIM = 128
SEQ_LEN = 32768
GROUP = 10
TOK_DEV = 32


def rotate_heads(joined, first_col, position, sign):
    rows, cols = joined.shape
    heads = cols // HEAD_DIM
    half = HEAD_DIM // 2
    parts = joined.reshape(rows, heads, 2, half)
    inverse = jnp.exp(
        -jnp.log(jnp.float32(1000000.0)) * (2.0 * jnp.arange(half).astype(jnp.float32) / HEAD_DIM)
    )
    angle = position.astype(jnp.float32)[:, None] * inverse[None, :]
    cosine = jnp.cos(angle)[:, None, :]
    sine = sign * jnp.sin(angle)[:, None, :]
    first = parts[:, :, 0, :]
    second = parts[:, :, 1, :]
    turned = jnp.stack([first * cosine - second * sine, second * cosine + first * sine], axis=2)
    head_index = first_col // HEAD_DIM + jnp.arange(heads)
    rotated = head_index % GROUP != GROUP - 1
    result = jnp.where(rotated[None, :, None, None], turned, parts)
    return result.reshape(rows, cols)


def positions(rows, stride):
    row_index = jnp.arange(rows)
    return row_index // TOK_DEV * stride + row_index % TOK_DEV


def normalize(tokens, norm_gain):
    values = tokens.astype(jnp.float32)
    scale = lax.rsqrt(jnp.mean(values * values, axis=1, keepdims=True) + 1e-06)
    return (values * scale * norm_gain[None, :]).astype(jnp.bfloat16)


def shards(tokens, norm_gain, qkv_weight, qkv_bias, qkv_grad):
    width = qkv_weight.shape[1]
    first_col = lax.axis_index("mp") * width
    stride = SEQ_LEN // lax.axis_size("mp")
    place = positions(qkv_grad.shape[0], stride)
    joined_grad = rotate_heads(qkv_grad.astype(jnp.float32), first_col, place, -1.0)
    bias_grad = jnp.sum(joined_grad, axis=0)
    joined_low = joined_grad.astype(jnp.bfloat16)
    normed_grad = lax.psum_scatter(
        lax.dot_general(
            joined_low, qkv_weight, (((1,), (1,)), ((), ())), preferred_element_type=jnp.float32
        ),
        "mp",
        scatter_dimension=0,
        tiled=True,
    )
    values = tokens.astype(jnp.float32)
    scale = lax.rsqrt(jnp.mean(values * values, axis=1, keepdims=True) + 1e-06)
    gain_grad = lax.psum(jnp.sum(normed_grad * values * scale, axis=0), "mp")
    inner = jnp.mean(norm_gain[None, :] * normed_grad * values, axis=1, keepdims=True)
    tokens_grad = scale * norm_gain[None, :] * normed_grad - values * scale * scale * scale * inner
    tokens_grad, gain_grad, bias_grad = (tokens_grad, gain_grad, bias_grad)
    tokens_grad, later = lax.optimization_barrier((tokens_grad, tokens))
    normed = normalize(later, norm_gain)
    project_normed = lax.all_gather(normed, "mp", axis=0, tiled=True)
    joined = (
        jnp.dot(project_normed, qkv_weight, preferred_element_type=jnp.float32) + qkv_bias[None, :]
    )
    place = positions(project_normed.shape[0], stride)
    qkv = rotate_heads(joined, first_col, place, 1.0).astype(jnp.bfloat16)
    return (qkv, tokens_grad, gain_grad, bias_grad)


def solution(mesh):
    in_specs = (P(("dp", "mp"), None), P(), P(None, "mp"), P("mp"), P("dp", "mp"))
    out_specs = (P("dp", "mp"), P(("dp", "mp"), None), P("dp"), P(("dp", "mp")))
    return jax.shard_map(shards, mesh=mesh, in_specs=in_specs, out_specs=out_specs, check_vma=False)
```

profile of v0, /device:TPU:0, one launch (start us, length us, event | category | flops | bytes accessed | tf_op | source)
XLA Modules:
  0.0 186.8 jit_solution(11591648086676076548)
XLA Ops:
  7.3 0.1 broadcast_in_dim.15
  7.4 0.1 broadcast_in_dim.16
  7.5 1.3 copy.9
  8.8 0.2 multiply_sine_fusion
  9.0 0.2 multiply_subtract_fusion.1
  9.2 0.1 pad_maximum_fusion
  9.4 0.4 copy.10
  9.8 0.7 copy-done.1
  10.5 20.4 %fusion.11 = f32[128,8192]{1,0:T(8,128)} fusion(bf16[8192,2560]{1,0:T(8,128)(2,1)} %param.7, f32[128,2560]{1,0:T(8,128)S(1)} %copy.10, pred[2560]{0:T(1024)(128)(4,1)S(1)} %broadcast_in_dim.16, bf16[128,2560]{1,0:T(8,128)(2,1)S(1)} %copy-done.1), kind=kOutput, calls=%fused_computation.23 | convolution fusion | flops 5369364480 | bytes 48105984 | tf_op jit(solution)/shard_map/dot_general | solution.py:52
  31.0 1.0 copy-done
  32.0 0.2 fusion.3
  32.2 78.4 %reduce-scatter.2.cloned.1.call-done = f32[32,8192]{1,0:T(8,128)} async-done(((f32[128,8192]{1,0:T(8,128)}), f32[32,8192]{1,0:T(8,128)}) %reduce-scatter.2.cloned.1.call-update) | async-done | bytes 1048592 | tf_op jit(solution)/shard_map/reduce_scatter | solution.py:51
  110.6 1.7 fusion.10
  112.3 1.3 fusion.7
  113.7 0.2 fusion
  113.9 1.0 fusion.2
  114.9 0.8 fusion.13
  115.7 19.8 %psum.7 = f32[8192]{0:T(1024)} all-reduce(f32[8192]{0:T(1024)S(1)} %get-tuple-element.8), channel_id=1, replica_groups=mesh['dp'=8,'mp'=4] {'mp'}, use_global_device_ids=true, to_apply=%region_5.6 | all-reduce | flops 8192 | bytes 65536 | tf_op jit(solution)/shard_map/psum | solution.py:61
  135.5 26.1 %all-gather.2.cloned.1.call-done = bf16[128,8192]{1,0:T(8,128)(2,1)} async-done(((bf16[32,8192]{1,0:T(8,128)(2,1)}), bf16[128,8192]{1,0:T(8,128)(2,1)}) %all-gather.2.cloned.1.call-update) | async-done | bytes 2097168 | tf_op jit(solution)/shard_map/all_gather | solution.py:67
  161.6 16.4 %convolution_add_fusion = f32[128,2560]{1,0:T(8,128)S(1)} fusion(bf16[128,8192]{1,0:T(8,128)(2,1)} %all-gather.2.cloned.1.call-done, bf16[8192,2560]{1,0:T(8,128)(2,1)} %param.7, f32[2560]{0:T(1024)S(1)} %copy-done.4), kind=kOutput, calls=%fused_computation | convolution fusion | flops 5369036800 | bytes 45361152 | tf_op jit(solution)/shard_map/dot_general | solution.py:69
  178.0 0.4 copy.11
  178.4 0.2 multiply_subtract_fusion
  178.7 0.2 copy.12
  179.0 1.0 select_convert_fusion
  (19 shorter events, 0.2 us)
Async XLA Ops:
  7.2 103.4 %reduce-scatter.2.cloned.1.call-start = ((), (), s32[]{:S(2)}) async-start(), calls=%async_computation.1 | async-start | bytes 5242880 | tf_op jit(solution)/shard_map/reduce_scatter | solution.py:51
  9.4 1.1 copy-start.1
  30.9 1.0 copy-start
  30.9 79.7 %copy-start.3 = (f32[8192]{0:T(1024)S(1)}, f32[8192]{0:T(1024)}, u32[]{:S(2)}) copy-start(f32[8192]{0:T(1024)} %param.6) | copy-start | bytes 98308
  30.9 130.7 %all-gather.2.cloned.1.call-start = ((), (), s32[]{:S(2)}) async-start(), calls=%async_computation.2 | async-start | bytes 2621440 | tf_op jit(solution)/shard_map/all_gather | solution.py:67
  110.6 1.7 copy-start.2
  114.9 46.7 %copy-start.4 = (f32[2560]{0:T(1024)S(1)}, f32[2560]{0:T(1024)}, u32[]{:S(2)}) copy-start(f32[2560]{0:T(1024)} %param.8) | copy-start | bytes 30724
Sparse Core Ops, SparseCore 0:
  31.1 79.5 reduce-scatter.1
  115.0 46.5 all-gather.1
where the time goes:
time: 187 us
  waiting for transfers between devices  105 us (56%)
  matrix products  36.9 us (20%)
  blocking collectives  19.8 us (11%)
  between operations  14.2 us (8%)
  other arithmetic  7.08 us (4%)
  local copies, waits for them, and re-layouts  4.19 us (2%)
    reduce_scatter x1, waiting for transfers between devices, shards(): lax.psum_scatter(lax.dot_general(joined_low, qkv_weight, (((1,), (1,)), (...  78.4 us
    all_gather x1, waiting for transfers between devices, shards(): project_normed = lax.all_gather(normed, 'mp', axis=0, tiled=True)  26.1 us
    dot_general x1, matrix products, shards(): lax.dot_general(joined_low, qkv_weight, (((1,), (1,)), ((), ())), preferr...  20.4 us
    psum x1, blocking collectives, shards(): gain_grad = lax.psum(jnp.sum(normed_grad * values * scale, axis=0), 'mp')  19.8 us
    dot_general x1, matrix products, shards(): jnp.dot(project_normed, qkv_weight, preferred_element_type=jnp.float32)  16.4 us
  transfers between devices with their start and end apart: 2, of which 2 were waited for; matrix products, arithmetic and copies ran while one was open for 1% of the time, Pallas kernels for 0%

commit v1 on v0

--- a/solution.py
+++ b/solution.py
@@ -58,7 +58,9 @@
     )
     values = tokens.astype(jnp.float32)
     scale = lax.rsqrt(jnp.mean(values * values, axis=1, keepdims=True) + 1e-06)
-    gain_grad = lax.psum(jnp.sum(normed_grad * values * scale, axis=0), "mp")
+    block = jnp.sum(normed_grad * values * scale, axis=0)
+    pieces = lax.all_gather(block, "mp")
+    gain_grad = jnp.sum(pieces, axis=0)
     inner = jnp.mean(norm_gain[None, :] * normed_grad * values, axis=1, keepdims=True)
     tokens_grad = scale * norm_gain[None, :] * normed_grad - values * scale * scale * scale * inner
     tokens_grad, gain_grad, bias_grad = (tokens_grad, gain_grad, bias_grad)

time: 187 us -> 187 us (level)
  blocking collectives: 19.8 us -> 14.5 us
  waiting for transfers between devices: 105 us -> 109 us
    psum x1 -> x0, blocking collectives: 19.8 us -> none  [shards(): gain_grad = lax.psum(jnp.sum(normed_grad * values * scale, axis=0), 'mp')]
    all_gather x0 -> x1, blocking collectives: none -> 14.5 us  [shards(): pieces = lax.all_gather(block, 'mp')]
    all_gather x1, waiting for transfers between devices: 26.1 us -> 30.7 us  [shards(): project_normed = lax.all_gather(normed, 'mp', axis=0, tiled=True)]
where the time goes in v1:
time: 187 us
  waiting for transfers between devices  109 us (58%)
  matrix products  36.9 us (20%)
  blocking collectives  14.5 us (8%)
  between operations  14.2 us (8%)
  other arithmetic  7.77 us (4%)
  local copies, waits for them, and re-layouts  4.24 us (2%)
    reduce_scatter x1, waiting for transfers between devices, shards(): lax.psum_scatter(lax.dot_general(joined_low, qkv_weight, (((1,), (1,)), (...  78.4 us
    all_gather x1, waiting for transfers between devices, shards(): project_normed = lax.all_gather(normed, 'mp', axis=0, tiled=True)  30.7 us
    dot_general x1, matrix products, shards(): lax.dot_general(joined_low, qkv_weight, (((1,), (1,)), ((), ())), preferr...  20.4 us
    dot_general x1, matrix products, shards(): jnp.dot(project_normed, qkv_weight, preferred_element_type=jnp.float32)  16.4 us
    all_gather x1, blocking collectives, shards(): pieces = lax.all_gather(block, 'mp')  14.5 us
  transfers between devices with their start and end apart: 2, of which 2 were waited for; matrix products, arithmetic and copies ran while one was open for 1% of the time, Pallas kernels for 0%

profile of v1, /device:TPU:0, one launch (start us, length us, event | category | flops | bytes accessed | tf_op | source)
XLA Modules:
  0.0 186.8 jit_solution(6070158731925100734)
XLA Ops:
  7.4 0.1 broadcast_in_dim.16
  7.5 1.3 copy.17
  8.8 0.2 multiply_sine_fusion
  9.0 0.2 multiply_subtract_fusion.1
  9.2 0.1 pad_maximum_fusion
  9.4 0.4 copy.18
  9.8 0.7 copy-done.1
  10.5 20.4 %fusion.11 = f32[128,8192]{1,0:T(8,128)} fusion(bf16[8192,2560]{1,0:T(8,128)(2,1)} %param.7, f32[128,2560]{1,0:T(8,128)S(1)} %copy.18, pred[2560]{0:T(1024)(128)(4,1)S(1)} %broadcast_in_dim.16, bf16[128,2560]{1,0:T(8,128)(2,1)S(1)} %copy-done.1), kind=kOutput, calls=%fused_computation.23 | convolution fusion | flops 5369364480 | bytes 48105984 | tf_op jit(solution)/shard_map/dot_general | solution.py:52
  31.0 1.0 copy-done
  32.0 0.2 fusion.3
  32.2 78.4 %reduce-scatter.2.cloned.1.call-done = f32[32,8192]{1,0:T(8,128)} async-done(((f32[128,8192]{1,0:T(8,128)}), f32[32,8192]{1,0:T(8,128)}) %reduce-scatter.2.cloned.1.call-update) | async-done | bytes 1048592 | tf_op jit(solution)/shard_map/reduce_scatter | solution.py:51
  110.6 1.7 fusion.10
  112.3 1.3 fusion.7
  113.7 0.2 fusion
  113.9 1.0 fusion.2
  114.9 0.8 fusion.13
  115.7 14.5 %all-gather = f32[32768]{0:T(1024)S(1)} all-gather(f32[8192]{0:T(1024)S(1)} %get-tuple-element.8), channel_id=2, replica_groups=mesh['dp'=8,'mp'=4] {'mp'}, dimensions={0}, use_global_device_ids=true | all-gather | bytes 163840 | tf_op jit(solution)/shard_map/all_gather | solution.py:62
  130.2 0.7 reduce_sum.58
  130.9 30.7 %all-gather.3.cloned.1.call-done = bf16[128,8192]{1,0:T(8,128)(2,1)} async-done(((bf16[32,8192]{1,0:T(8,128)(2,1)}), bf16[128,8192]{1,0:T(8,128)(2,1)}) %all-gather.3.cloned.1.call-update) | async-done | bytes 2097168 | tf_op jit(solution)/shard_map/all_gather | solution.py:69
  161.6 16.4 %convolution_add_fusion = f32[128,2560]{1,0:T(8,128)S(1)} fusion(bf16[128,8192]{1,0:T(8,128)(2,1)} %all-gather.3.cloned.1.call-done, bf16[8192,2560]{1,0:T(8,128)(2,1)} %param.7, f32[2560]{0:T(1024)S(1)} %copy-done.4), kind=kOutput, calls=%fused_computation | convolution fusion | flops 5369036800 | bytes 45361152 | tf_op jit(solution)/shard_map/dot_general | solution.py:71
  178.0 0.4 copy.19
  178.4 0.2 multiply_subtract_fusion
  178.7 0.2 copy.20
  179.0 1.0 select_convert_fusion
  (21 shorter events, 0.4 us)
Async XLA Ops:
  7.2 103.4 %reduce-scatter.2.cloned.1.call-start = ((), (), s32[]{:S(2)}) async-start(), calls=%async_computation.1 | async-start | bytes 5242880 | tf_op jit(solution)/shard_map/reduce_scatter | solution.py:51
  9.4 1.1 copy-start.1
  30.9 1.0 copy-start
  30.9 79.7 %copy-start.3 = (f32[8192]{0:T(1024)S(1)}, f32[8192]{0:T(1024)}, u32[]{:S(2)}) copy-start(f32[8192]{0:T(1024)} %param.6) | copy-start | bytes 98308
  30.9 130.7 %all-gather.3.cloned.1.call-start = ((), (), s32[]{:S(2)}) async-start(), calls=%async_computation.2 | async-start | bytes 2621440 | tf_op jit(solution)/shard_map/all_gather | solution.py:69
  110.6 1.7 copy-start.2
  114.9 46.7 %copy-start.4 = (f32[2560]{0:T(1024)S(1)}, f32[2560]{0:T(1024)}, u32[]{:S(2)}) copy-start(f32[2560]{0:T(1024)} %param.8) | copy-start | bytes 30724
Sparse Core Ops, SparseCore 0:
  31.1 79.5 reduce-scatter.1
  115.0 46.5 all-gather.2
